TPU v7x, 16 devices: a whole 2x2x2 slice. The times are simulated.
16 devices in a mesh: dp: 4 (over z, y), sp: 4 (over x, core).
Axes of the slice: x: 2, y: 2, z: 2, core: 2. Of those that a mesh axis runs over, the one named last changes fastest.
Arguments:
- images: bfloat16 [64, 16, 512, 256], P('dp', 'sp'), parts along dimension 0
- w_a: bfloat16 [4, 3, 3, 256, 256], replicated
- bn_a: float32 [4, 2, 256], replicated
- w_down: bfloat16 [3, 3, 256, 2048], replicated
- bn_down: float32 [2, 2048], replicated
- w_in: bfloat16 [2, 2048, 512], replicated
- bn_in: float32 [2, 2, 512], replicated
- w_mid: bfloat16 [2, 3, 3, 512, 512], replicated
- bn_mid: float32 [2, 2, 512], replicated
- w_out: bfloat16 [2, 512, 2048], replicated
- bn_out: float32 [2, 2, 2048], replicated
Outputs:
- output: bfloat16 [64, 8, 256, 2048], P('dp', 'sp'), parts along dimension 0
There are 4 independent parts. A program takes and returns all parts, laid end to end along the dimension named above; an argument that names none is the same for every part.
All inputs are finite; a program needn't handle non-finite values.
Results may differ from a plain program's by a relative error of at most 0.02.
Values are sent between devices in bfloat16 or wider.
A program may use at most 1 GiB of HBM per device.

v0:
```python
import jax
import jax.numpy as jnp
from jax import lax
from jax.sharding import PartitionSpec as P, NamedSharding

NORM_EPS = 1e-5
CONV_DIMS = ("NHWC", "HWIO", "NHWC")


def solution(mesh):
    groups = mesh.shape["sp"]
    to_next = [(device, device + 1) for device in range(groups - 1)]
    to_prev = [(device + 1, device) for device in range(groups - 1)]

    def conv_same(hidden, weight):
        from_above = lax.ppermute(hidden[:, -1:], "sp", to_next)
        from_below = lax.ppermute(hidden[:, :1], "sp", to_prev)
        padded = jnp.concatenate([from_above, hidden, from_below], axis=1)
        return lax.conv_general_dilated(padded, weight, (1, 1), ((0, 0), (1, 1)), dimension_numbers=CONV_DIMS, preferred_element_type=jnp.float32)

    def conv_down(hidden, weight):
        from_below = lax.ppermute(hidden[:, :1], "sp", to_prev)
        padded = jnp.concatenate([hidden, from_below], axis=1)
        return lax.conv_general_dilated(padded, weight, (2, 2), ((0, 0), (0, 1)), dimension_numbers=CONV_DIMS, preferred_element_type=jnp.float32)

    def conv_point(hidden, weight):
        return jnp.einsum("bhwc,cd->bhwd", hidden, weight, preferred_element_type=jnp.float32)

    def batch_norm(pre_act, params):
        norm_count = pre_act.shape[0] * pre_act.shape[1] * pre_act.shape[2] * groups
        part_sums = jnp.stack([jnp.sum(pre_act, axis=(0, 1, 2)), jnp.sum(pre_act * pre_act, axis=(0, 1, 2))])
        group_moments = lax.psum(part_sums, "sp") / norm_count
        chan_mean = group_moments[0]
        chan_var = group_moments[1] - chan_mean * chan_mean
        chan_scale = params[0] * lax.rsqrt(chan_var + NORM_EPS)
        return (pre_act - chan_mean) * chan_scale + params[1]

    def norm_relu(pre_act, params):
        return jax.nn.relu(batch_norm(pre_act, params)).astype(jnp.bfloat16)

    def forward(images, w_a, bn_a, w_down, bn_down, w_in, bn_in, w_mid, bn_mid, w_out, bn_out):
        hidden = images
        for layer_num in range(w_a.shape[0]):
            hidden = norm_relu(conv_same(hidden, w_a[layer_num]), bn_a[layer_num])
        hidden = norm_relu(conv_down(hidden, w_down), bn_down)
        for block_num in range(w_in.shape[0]):
            branch = norm_relu(conv_point(hidden, w_in[block_num]), bn_in[block_num])
            branch = norm_relu(conv_same(branch, w_mid[block_num]), bn_mid[block_num])
            summed = batch_norm(conv_point(branch, w_out[block_num]), bn_out[block_num]) + hidden
            hidden = jax.nn.relu(summed).astype(jnp.bfloat16)
        return hidden

    act_spec = P("dp", "sp", None, None)
    return jax.shard_map(forward, mesh=mesh, in_specs=(act_spec,) + (P(),) * 10, out_specs=act_spec, check_vma=False)
```

profile of v0, /device:TPU:0, one launch (start us, length us, event | category | flops | bytes accessed | tf_op | source)
XLA Modules:
  0.0 1379.5 jit_solution(54827855921465232)
XLA Ops:
  0.0 15.5 %copy.12 = bf16[16,4,512,256]{3,0,2,1:T(8,128)(2,1)S(1)} copy(bf16[16,4,512,256]{3,2,1,0:T(8,128)(2,1)} %param.11) | data formatting | bytes 33554432 | tf_op args[0]
  16.1 2.9 collective-permute-start
  22.3 3.2 collective-permute-done
  25.5 4.3 collective-permute-done.1
  29.8 48.4 %fusion.99 = (f32[256]{0:T(256)S(1)}, f32[256]{0:T(256)S(1)}, f32[16,4,512,256]{3,0,2,1:T(8,128)}) fusion(bf16[16,1,512,256]{3,0,2,1:T(8,128)(2,1)} %collective-permute-done.1, bf16[16,4,512,256]{3,0,2,1:T(8,128)(2,1)S(1)} %copy.12, bf16[16,1,512,256]{3,0,2,1:T(8,128)(2,1)S(1)} %collective-permute-done, bf16[3,3,256,256]{3,2,1,0:T(8,128)(2,1)S(1)} %fusion.81.clone.5), kind=kOutput, calls=%fused_computation.154 | convolution fusion | flops 38705037312 | bytes 59901952 | tf_op jit(solution)/shard_map/conv_general_dilated | solution.py:19
  78.3 47.2 %psum.77 = f32[2,256]{1,0:T(2,128)S(1)} all-reduce(f32[2,256]{1,0:T(2,128)S(1)} %pad_maximum_fusion.9), channel_id=1, replica_groups=mesh['dp'=4,'sp'=4] {'sp'}, use_global_device_ids=true, to_apply=%region_2.0 | all-reduce | flops 512 | bytes 4096 | tf_op jit(solution)/shard_map/psum | solution.py:32
  125.5 13.8 maximum_convert_fusion.4
  144.2 3.8 collective-permute-done.2
  148.0 4.0 collective-permute-done.3
  152.0 48.4 %fusion.98 = (f32[256]{0:T(256)S(1)}, f32[256]{0:T(256)S(1)}, f32[16,4,512,256]{3,0,2,1:T(8,128)}) fusion(bf16[16,1,512,256]{3,0,2,1:T(8,128)(2,1)} %collective-permute-done.3, bf16[16,4,512,256]{3,0,2,1:T(8,128)(2,1)S(1)} %maximum_convert_fusion.4, bf16[16,1,512,256]{3,0,2,1:T(8,128)(2,1)S(1)} %collective-permute-done.2, ...), kind=kOutput, calls=%fused_computation.153 | convolution fusion | flops 38705037312 | bytes 59901952 | tf_op jit(solution)/shard_map/conv_general_dilated | solution.py:19
  200.5 47.0 %psum.78 = f32[2,256]{1,0:T(2,128)S(1)} all-reduce(f32[2,256]{1,0:T(2,128)S(1)} %pad_maximum_fusion.10), channel_id=1, replica_groups=mesh['dp'=4,'sp'=4] {'sp'}, use_global_device_ids=true, to_apply=%region_5.6 | all-reduce | flops 512 | bytes 4096 | tf_op jit(solution)/shard_map/psum | solution.py:32
  247.5 13.8 maximum_convert_fusion.3
  266.6 3.4 collective-permute-done.4
  270.0 4.4 collective-permute-done.5
  274.5 48.4 %fusion.97 = (f32[256]{0:T(256)S(1)}, f32[256]{0:T(256)S(1)}, f32[16,4,512,256]{3,0,2,1:T(8,128)}) fusion(bf16[16,1,512,256]{3,0,2,1:T(8,128)(2,1)} %collective-permute-done.5, bf16[16,4,512,256]{3,0,2,1:T(8,128)(2,1)S(1)} %maximum_convert_fusion.3, bf16[16,1,512,256]{3,0,2,1:T(8,128)(2,1)S(1)} %collective-permute-done.4, ...), kind=kOutput, calls=%fused_computation.152 | convolution fusion | flops 38705037312 | bytes 59901952 | tf_op jit(solution)/shard_map/conv_general_dilated | solution.py:19
  322.9 47.0 %psum.79 = f32[2,256]{1,0:T(2,128)S(1)} all-reduce(f32[2,256]{1,0:T(2,128)S(1)} %pad_maximum_fusion.11), channel_id=1, replica_groups=mesh['dp'=4,'sp'=4] {'sp'}, use_global_device_ids=true, to_apply=%region_8.9 | all-reduce | flops 512 | bytes 4096 | tf_op jit(solution)/shard_map/psum | solution.py:32
  369.9 13.8 maximum_convert_fusion.2
  388.8 3.6 collective-permute-done.6
  392.4 4.0 collective-permute-done.7
  396.5 48.4 %fusion.96 = (f32[256]{0:T(256)S(1)}, f32[256]{0:T(256)S(1)}, f32[16,4,512,256]{3,0,2,1:T(8,128)}) fusion(bf16[16,1,512,256]{3,0,2,1:T(8,128)(2,1)} %collective-permute-done.7, bf16[16,4,512,256]{3,0,2,1:T(8,128)(2,1)S(1)} %maximum_convert_fusion.2, bf16[16,1,512,256]{3,0,2,1:T(8,128)(2,1)S(1)} %collective-permute-done.6, ...), kind=kOutput, calls=%fused_computation.151 | convolution fusion | flops 38705037312 | bytes 59901952 | tf_op jit(solution)/shard_map/conv_general_dilated | solution.py:19
  444.9 47.0 %psum.80 = f32[2,256]{1,0:T(2,128)S(1)} all-reduce(f32[2,256]{1,0:T(2,128)S(1)} %pad_maximum_fusion.12), channel_id=1, replica_groups=mesh['dp'=4,'sp'=4] {'sp'}, use_global_device_ids=true, to_apply=%region_11.12 | all-reduce | flops 512 | bytes 4096 | tf_op jit(solution)/shard_map/psum | solution.py:32
  492.0 13.8 maximum_convert_fusion.1
  505.7 6.2 copy-done
  515.1 6.1 collective-permute-done.8
  521.2 88.1 %fusion.95 = (f32[2048]{0:T(1024)S(1)}, f32[2048]{0:T(1024)S(1)}, f32[16,2,256,2048]{3,0,2,1:T(8,128)}) fusion(bf16[3,3,256,2048]{3,2,1,0:T(8,128)(2,1)} %param.14, bf16[16,1,512,256]{3,0,2,1:T(8,128)(2,1)S(1)} %collective-permute-done.8, bf16[16,4,512,256]{3,0,2,1:T(8,128)(2,1)} %copy-done), kind=kOutput, calls=%fused_computation.150 | convolution fusion | flops 77301022720 | bytes 97533952 | tf_op jit(solution)/shard_map/conv_general_dilated | solution.py:24
  609.4 50.8 %psum.81 = f32[2,2048]{1,0:T(2,128)S(1)} all-reduce(f32[2,2048]{1,0:T(2,128)S(1)} %pad_maximum_fusion.2), channel_id=1, replica_groups=mesh['dp'=4,'sp'=4] {'sp'}, use_global_device_ids=true, to_apply=%region_14.15 | all-reduce | flops 4096 | bytes 32768 | tf_op jit(solution)/shard_map/psum | solution.py:32
  660.3 33.2 %maximum_convert_fusion = bf16[16,2,256,2048]{3,0,2,1:T(8,128)(2,1)} fusion(f32[16,2,256,2048]{3,0,2,1:T(8,128)} %get-tuple-element.87, f32[2048]{0:T(1024)S(1)} %bitcast.157, f32[2048]{0:T(1024)S(1)} %rsqrt_multiply_fusion.2, f32[2048]{0:T(1024)S(1)} %bitcast.155), kind=kLoop, calls=%fused_computation.14 | loop fusion | flops 83886080 | bytes 100687872 | tf_op jit(solution)/shard_map/convert_element_type | solution.py:39
  693.5 66.5 %fusion.103 = (f32[512]{0:T(512)S(1)}, f32[512]{0:T(512)S(1)}, f32[16,2,256,512]{3,2,1,0:T(8,128)}) fusion(bf16[2,2048,512]{2,1,0:T(8,128)(2,1)} %param.16, bf16[16,2,256,2048]{3,0,2,1:T(8,128)(2,1)} %maximum_convert_fusion), kind=kOutput, calls=%fused_computation.158 | convolution fusion | flops 17192452096 | bytes 52432896 | tf_op jit(solution)/shard_map/bhwc,cd->bhwd/dot_general | solution.py:27
  760.1 5.7 psum.82
  765.8 7.6 maximum_convert_fusion.6
  778.8 4.0 collective-permute-done.9
  782.8 3.8 collective-permute-done.10
  788.5 77.2 %fusion.102 = (f32[512]{0:T(512)S(1)}, f32[512]{0:T(512)S(1)}, f32[16,2,256,512]{3,0,2,1:T(8,128)}) fusion(bf16[2,3,3,512,512]{4,3,2,1,0:T(8,128)(2,1)} %param.18, bf16[16,4,256,512]{3,2,1,0:T(8,128)(2,1)S(1)} %pad_maximum_fusion), kind=kOutput, calls=%fused_computation.157 | convolution fusion | flops 38566625280 | bytes 38277120 | tf_op jit(solution)/shard_map/conv_general_dilated | solution.py:19
  865.7 46.9 %psum.83 = f32[2,512]{1,0:T(2,128)S(1)} all-reduce(f32[2,512]{1,0:T(2,128)S(1)} %pad_maximum_fusion.6), channel_id=1, replica_groups=mesh['dp'=4,'sp'=4] {'sp'}, use_global_device_ids=true, to_apply=%region_20.21 | all-reduce | flops 1024 | bytes 8192 | tf_op jit(solution)/shard_map/psum | solution.py:32
  912.7 36.6 %fusion.94 = (f32[2048]{0:T(1024)S(1)}, f32[2048]{0:T(1024)S(1)}, f32[16,2,256,2048]{3,2,1,0:T(8,128)}) fusion(bf16[2,512,2048]{2,1,0:T(8,128)(2,1)} %param.20, f32[16,2,256,512]{3,0,2,1:T(8,128)} %get-tuple-element.89, f32[512]{0:T(512)S(1)} %bitcast.224, f32[512]{0:T(512)S(1)} %rsqrt_multiply_fusion.5, f32[512]{0:T(512)S(1)} %bitcast.194), kind=kOutput, calls=%fused_computation.149 | convolution fusion | flops 17251168256 | bytes 86005760 | tf_op jit(solution)/shard_map/bhwc,cd->bhwd/dot_general | solution.py:27
  949.3 10.1 psum.84
  959.5 63.4 %fusion.9 = bf16[16,2,256,2048]{3,0,2,1:T(8,128)(2,1)} fusion(f32[16,2,256,2048]{3,2,1,0:T(8,128)} %get-tuple-element.90, f32[2048]{0:T(1024)S(1)} %bitcast.164, f32[2048]{0:T(1024)S(1)} %rsqrt_multiply_fusion.1, f32[2048]{0:T(1024)S(1)} %bitcast.160, f32[2048]{0:T(1024)S(1)} %bitcast.158, f32[2048]{0:T(1024)S(1)} %copy-done.6, ...), kind=kLoop, calls=%fused_computation.11 | loop fusion | flops 201326592 | bytes 167821312 | tf_op jit(solution)/shard_map/convert_element_type | solution.py:50
  1022.9 66.5 %fusion.101 = (f32[512]{0:T(512)S(1)}, f32[512]{0:T(512)S(1)}, f32[16,2,256,512]{3,2,1,0:T(8,128)}) fusion(bf16[2,2048,512]{2,1,0:T(8,128)(2,1)} %param.16, bf16[16,2,256,2048]{3,0,2,1:T(8,128)(2,1)} %fusion.9), kind=kOutput, calls=%fused_computation.156 | convolution fusion | flops 17192452096 | bytes 52432896 | tf_op jit(solution)/shard_map/bhwc,cd->bhwd/dot_general | solution.py:27
  1089.4 5.7 psum.85
  1095.1 7.6 maximum_convert_fusion.5
  1106.9 5.2 collective-permute-done.11
  1112.1 3.8 collective-permute-done.12
  1117.9 77.0 %fusion.100 = (f32[512]{0:T(512)S(1)}, f32[512]{0:T(512)S(1)}, f32[16,2,256,512]{3,0,2,1:T(8,128)}) fusion(bf16[2,3,3,512,512]{4,3,2,1,0:T(8,128)(2,1)} %param.18, bf16[16,4,256,512]{3,2,1,0:T(8,128)(2,1)S(1)} %pad_maximum_fusion.1), kind=kOutput, calls=%fused_computation.155 | convolution fusion | flops 38566625280 | bytes 38277120 | tf_op jit(solution)/shard_map/conv_general_dilated | solution.py:19
  1194.9 46.9 %psum.86 = f32[2,512]{1,0:T(2,128)S(1)} all-reduce(f32[2,512]{1,0:T(2,128)S(1)} %pad_maximum_fusion.8), channel_id=1, replica_groups=mesh['dp'=4,'sp'=4] {'sp'}, use_global_device_ids=true, to_apply=%region_29.30 | all-reduce | flops 1024 | bytes 8192 | tf_op jit(solution)/shard_map/psum | solution.py:32
  1241.9 36.5 %fusion.93 = (f32[2048]{0:T(1024)S(1)}, f32[2048]{0:T(1024)S(1)}, f32[16,2,256,2048]{3,2,1,0:T(8,128)}) fusion(bf16[2,512,2048]{2,1,0:T(8,128)(2,1)} %param.20, f32[16,2,256,512]{3,0,2,1:T(8,128)} %get-tuple-element.92, f32[512]{0:T(512)S(1)} %bitcast.223, f32[512]{0:T(512)S(1)} %rsqrt_multiply_fusion.3, f32[512]{0:T(512)S(1)} %bitcast.192), kind=kOutput, calls=%fused_computation.148 | convolution fusion | flops 17251168256 | bytes 86005760 | tf_op jit(solution)/shard_map/bhwc,cd->bhwd/dot_general | solution.py:27
  1278.5 10.1 psum.87
  1288.6 60.3 %fusion.4 = bf16[16,2,256,2048]{3,0,2,1:T(8,128)(2,1)} fusion(f32[16,2,256,2048]{3,2,1,0:T(8,128)} %get-tuple-element.93, bf16[16,2,256,2048]{3,0,2,1:T(8,128)(2,1)} %fusion.9, f32[2048]{0:T(1024)S(1)} %bitcast.163, f32[2048]{0:T(1024)S(1)} %rsqrt_multiply_fusion, f32[2048]{0:T(1024)S(1)} %bitcast.162), kind=kLoop, calls=%fused_computation.5 | loop fusion | flops 117440512 | bytes 134242304 | tf_op jit(solution)/shard_map/convert_element_type | solution.py:50
  1349.0 30.2 %copy.23 = bf16[16,2,256,2048]{3,2,1,0:T(8,128)(2,1)} copy(bf16[16,2,256,2048]{3,0,2,1:T(8,128)(2,1)} %fusion.4) | data formatting | bytes 67108864 | tf_op jit(solution)/shard_map/convert_element_type | solution.py:50
  (127 shorter events, 36.3 us)
Async XLA Ops:
  15.5 4.8 copy-start.14
  16.1 9.4 collective-permute-start
  19.0 10.8 collective-permute-start.1
  139.9 8.1 collective-permute-start.2
  141.5 10.5 collective-permute-start.3
  144.2 103.3 %copy-start.25 = (f32[1,1,256]{2,1,0:T(1,128)S(1)}, f32[1,1,256]{2,1,0:T(1,128)}, u32[]{:S(2)}) copy-start(f32[1,1,256]{2,1,0:T(1,128)} %get-tuple-element.63) | copy-start | bytes 3076
  144.2 103.3 %copy-start.22 = (f32[1,1,256]{2,1,0:T(1,128)S(1)}, f32[1,1,256]{2,1,0:T(1,128)}, u32[]{:S(2)}) copy-start(f32[1,1,256]{2,1,0:T(1,128)} %get-tuple-element.62) | copy-start | bytes 3076
  261.9 8.1 collective-permute-start.4
  263.9 10.5 collective-permute-start.5
  266.6 103.3 %copy-start.24 = (f32[1,1,256]{2,1,0:T(1,128)S(1)}, f32[1,1,256]{2,1,0:T(1,128)}, u32[]{:S(2)}) copy-start(f32[1,1,256]{2,1,0:T(1,128)} %get-tuple-element.61) | copy-start | bytes 3076
  266.6 103.3 %copy-start.21 = (f32[1,1,256]{2,1,0:T(1,128)S(1)}, f32[1,1,256]{2,1,0:T(1,128)}, u32[]{:S(2)}) copy-start(f32[1,1,256]{2,1,0:T(1,128)} %get-tuple-element.60) | copy-start | bytes 3076
  384.3 8.1 collective-permute-start.6
  385.9 10.5 collective-permute-start.7
  388.8 103.1 %copy-start.23 = (f32[1,1,256]{2,1,0:T(1,128)S(1)}, f32[1,1,256]{2,1,0:T(1,128)}, u32[]{:S(2)}) copy-start(f32[1,1,256]{2,1,0:T(1,128)} %get-tuple-element.59) | copy-start | bytes 3076
  388.8 103.1 %copy-start.20 = (f32[1,1,256]{2,1,0:T(1,128)S(1)}, f32[1,1,256]{2,1,0:T(1,128)}, u32[]{:S(2)}) copy-start(f32[1,1,256]{2,1,0:T(1,128)} %get-tuple-element.66) | copy-start | bytes 3076
  491.9 21.9 %copy-start.15 = (f32[2,2,512]{2,1,0:T(2,128)S(1)}, f32[2,2,512]{2,1,0:T(2,128)}, u32[]{:S(2)}) copy-start(f32[2,2,512]{2,1,0:T(2,128)} %param.17) | copy-start | bytes 24580
  491.9 22.6 %copy-start.11 = (f32[2,2048]{1,0:T(2,128)S(1)}, f32[2,2048]{1,0:T(2,128)}, u32[]{:S(2)}) copy-start(f32[2,2048]{1,0:T(2,128)} %param.15) | copy-start | bytes 49156
  505.7 6.2 copy-start
  512.2 9.1 collective-permute-start.8
  521.2 139.0 %copy-start.9 = (f32[1,2048]{1,0:T(1,128)S(1)}, f32[1,2048]{1,0:T(1,128)}, u32[]{:S(2)}) copy-start(f32[1,2048]{1,0:T(1,128)} %get-tuple-element.49) | copy-start | bytes 24580
  521.2 139.0 %copy-start.3 = (f32[1,2048]{1,0:T(1,128)S(1)}, f32[1,2048]{1,0:T(1,128)}, u32[]{:S(2)}) copy-start(f32[1,2048]{1,0:T(1,128)} %get-tuple-element.50) | copy-start | bytes 24580
  660.2 33.3 %copy-start.1 = (f32[1,2048]{1,0:T(1,128)}, f32[1,2048]{1,0:T(1,128)S(1)}, u32[]{:S(2)}) copy-start(f32[1,2048]{1,0:T(1,128)S(1)} %get-tuple-element.47) | copy-start | bytes 24580
  660.2 33.3 %copy-start.5 = (f32[2048]{0:T(1024)}, f32[2048]{0:T(1024)S(1)}, u32[]{:S(2)}) copy-start(f32[2048]{0:T(1024)S(1)} %rsqrt_multiply_fusion.2) | copy-start | bytes 24580
  693.5 72.3 %copy-start.19 = (f32[1,1,512]{2,1,0:T(1,128)S(1)}, f32[1,1,512]{2,1,0:T(1,128)}, u32[]{:S(2)}) copy-start(f32[1,1,512]{2,1,0:T(1,128)} %get-tuple-element.57) | copy-start | bytes 6148
  693.5 72.3 %copy-start.13 = (f32[1,1,512]{2,1,0:T(1,128)S(1)}, f32[1,1,512]{2,1,0:T(1,128)}, u32[]{:S(2)}) copy-start(f32[1,1,512]{2,1,0:T(1,128)} %get-tuple-element.56) | copy-start | bytes 6148
  765.8 11.8 copy-start.16
  765.8 12.4 copy-start.8
  774.2 8.5 collective-permute-start.9
  776.3 10.3 collective-permute-start.10
  912.7 46.8 %copy-start.2 = (f32[1,2048]{1,0:T(1,128)S(1)}, f32[1,2048]{1,0:T(1,128)}, u32[]{:S(2)}) copy-start(f32[1,2048]{1,0:T(1,128)} %copy-done.1) | copy-start | bytes 24580
  912.7 46.8 %copy-start.4 = (f32[1,2048]{1,0:T(1,128)S(1)}, f32[1,2048]{1,0:T(1,128)}, u32[]{:S(2)}) copy-start(f32[1,2048]{1,0:T(1,128)} %get-tuple-element.50) | copy-start | bytes 24580
  912.7 46.8 %copy-start.6 = (f32[2048]{0:T(1024)S(1)}, f32[2048]{0:T(1024)}, u32[]{:S(2)}) copy-start(f32[2048]{0:T(1024)} %copy-done.5) | copy-start | bytes 24580
  1022.9 72.2 %copy-start.17 = (f32[1,1,512]{2,1,0:T(1,128)S(1)}, f32[1,1,512]{2,1,0:T(1,128)}, u32[]{:S(2)}) copy-start(f32[1,1,512]{2,1,0:T(1,128)} %get-tuple-element.55) | copy-start | bytes 6148
  1022.9 72.2 %copy-start.12 = (f32[1,1,512]{2,1,0:T(1,128)S(1)}, f32[1,1,512]{2,1,0:T(1,128)}, u32[]{:S(2)}) copy-start(f32[1,1,512]{2,1,0:T(1,128)} %get-tuple-element.58) | copy-start | bytes 6148
  1103.5 8.5 collective-permute-start.11
  1105.6 10.3 collective-permute-start.12
  1117.8 124.0 %copy-start.18 = (f32[1,1,512]{2,1,0:T(1,128)S(1)}, f32[1,1,512]{2,1,0:T(1,128)}, u32[]{:S(2)}) copy-start(f32[1,1,512]{2,1,0:T(1,128)} %get-tuple-element.51) | copy-start | bytes 6148
  1117.8 124.0 %copy-start.26 = (f32[1,1,512]{2,1,0:T(1,128)S(1)}, f32[1,1,512]{2,1,0:T(1,128)}, u32[]{:S(2)}) copy-start(f32[1,1,512]{2,1,0:T(1,128)} %get-tuple-element.54) | copy-start | bytes 6148
  1241.9 46.7 %copy-start.10 = (f32[1,1,2048]{2,1,0:T(1,128)S(1)}, f32[1,1,2048]{2,1,0:T(1,128)}, u32[]{:S(2)}) copy-start(f32[1,1,2048]{2,1,0:T(1,128)} %get-tuple-element.39) | copy-start | bytes 24580
  1241.9 46.8 %copy-start.7 = (f32[1,1,2048]{2,1,0:T(1,128)S(1)}, f32[1,1,2048]{2,1,0:T(1,128)}, u32[]{:S(2)}) copy-start(f32[1,1,2048]{2,1,0:T(1,128)} %get-tuple-element.42) | copy-start | bytes 24580
where the time goes:
time: 1390 us; the launch traced here: 1380 us
  matrix products  642 us (46%)
  blocking collectives  364 us (26%)
  other arithmetic  231 us (17%)
  local copies, waits for them, and re-layouts  64.8 us (5%)
  waiting for transfers between devices  53.7 us (4%)
  starting transfers between devices  21.9 us (2%)
    psum x11, blocking collectives, batch_norm(): group_moments = lax.psum(part_sums, 'sp') / norm_count  364 us
    conv_general_dilated x6, matrix products, conv_same(): lax.conv_general_dilated(padded, weight, (1, 1), ((0, 0), (1, 1)), dimens...  348 us
    dot_general x4, matrix products, conv_point(): jnp.einsum('bhwc,cd->bhwd', hidden, weight, preferred_element_type=jnp.fl...  206 us
    convert_element_type x2, other arithmetic, forward(): hidden = jax.nn.relu(summed).astype(jnp.bfloat16)  124 us
    convert_element_type x7, other arithmetic, norm_relu(): return jax.nn.relu(batch_norm(pre_act, params)).astype(jnp.bfloat16)  103 us
    conv_general_dilated x1, matrix products, conv_down(): lax.conv_general_dilated(padded, weight, (2, 2), ((0, 0), (0, 1)), dimens...  88.1 us
    convert_element_type x1, local copies, waits for them, and re-layouts, forward(): hidden = jax.nn.relu(summed).astype(jnp.bfloat16)  30.2 us
  transfers between devices with their start and end apart: 13, of which 13 were waited for; matrix products, arithmetic and copies ran while one was open for 1% of the time, Pallas kernels for 0%

commit v1 on v0

v1 whole, which is shorter than its diff:
```python
import functools

import jax
import jax.numpy as jnp
from jax import lax
from jax.experimental import pallas as pl
from jax.experimental.pallas import tpu as pltpu
from jax.sharding import PartitionSpec as P

NORM_EPS = 1e-5
BF, F32 = jnp.bfloat16, jnp.float32
TILE = 256
LEAD = 3
VMEM = 64000 * 1024


def coefficients(tot_ref, bn_ref, count):
    mean = tot_ref[0:1, :] / count
    var = tot_ref[1:2, :] / count - mean * mean
    return mean, bn_ref[0:1, :] * lax.rsqrt(var + NORM_EPS), bn_ref[1:2, :]


def normed(z, coef):
    if coef is None:
        return z.astype(F32)
    mean, scale, shift = coef
    return jnp.maximum((z - mean) * scale + shift, 0.0)


def column_sums(z):
    z3 = z.reshape(z.shape[0] // 8, 8, z.shape[1])
    return jnp.sum(z3, axis=0), jnp.sum(z3 * z3, axis=0)


def add_sums(st_ref, z, cols):
    first, second = column_sums(z)
    st_ref[0, :, cols] += first
    st_ref[1, :, cols] += second


def greet(n):
    me = lax.axis_index("sp")
    barrier = pltpu.get_barrier_semaphore()
    for d in range(1, n):
        pl.semaphore_signal(barrier, 1, device_id={"sp": lax.rem(me + d, n)}, device_id_type=pl.DeviceIdType.MESH)
    pl.semaphore_wait(barrier, n - 1)


def exchange_sums(n, st_ref, own, slots, send_sem, recv_sem, tot_ref):
    me = lax.axis_index("sp")
    own[2:8, :] = jnp.zeros((6, own.shape[1]), F32)
    own[0:1, :] = jnp.sum(st_ref[0], axis=0, keepdims=True)
    own[1:2, :] = jnp.sum(st_ref[1], axis=0, keepdims=True)
    copies = [
        pltpu.make_async_remote_copy(
            src_ref=own,
            dst_ref=slots.at[d - 1],
            send_sem=send_sem.at[d - 1],
            recv_sem=recv_sem.at[d - 1],
            device_id={"sp": lax.rem(me + d, n)},
            device_id_type=pl.DeviceIdType.MESH,
        )
        for d in range(1, n)
    ]
    for copy in copies:
        copy.start()
    for copy in copies:
        copy.wait()
    total = own[...]
    for d in range(n - 1):
        total = total + slots[d]
    tot_ref[...] = total


def shifted(hf):
    width = hf.shape[0]
    col = lax.broadcasted_iota(jnp.int32, hf.shape, 0)
    left = jnp.where(col == 0, 0.0, pltpu.roll(hf, 1, 0)).astype(BF)
    right = jnp.where(col == width - 1, 0.0, pltpu.roll(hf, width - 1, 0)).astype(BF)
    return left, right


def split_columns(hf, lanes, slot):
    width, chans = hf.shape
    for half in range(chans // 128):
        lanes[slot, half] = hf[:, half * 128 : (half + 1) * 128]
    return [
        jnp.concatenate([lanes[slot, half, pl.ds(parity, width // 2, stride=2), :] for half in range(chans // 128)], axis=1)
        for parity in range(2)
    ]


def halo_copy(sbuf, halo, send_sem, recv_sem, way, image, peer):
    return pltpu.make_async_remote_copy(
        src_ref=sbuf.at[way, image],
        dst_ref=halo.at[way, image],
        send_sem=send_sem.at[way, image],
        recv_sem=recv_sem.at[way, image],
        device_id={"sp": peer},
        device_id_type=pl.DeviceIdType.MESH,
    )


def conv_kernel(n, images, kind, normalize, count, *refs):
    refs = list(refs)
    xa_ref, xb_ref = refs.pop(0), refs.pop(0)
    edge_refs = [refs.pop(0) for _ in range(1 if kind == "down" else 2)]
    tot_in, bn_ref = (refs.pop(0), refs.pop(0)) if normalize else (None, None)
    w_ref, z_ref, tot_ref, buf0, buf1, sbuf, halo, st, own, slots, hs_sem, hr_sem, ss_sem, sr_sem, *rest = refs
    lanes = rest[0] if rest else None
    bufs = (buf0, buf1)
    t = pl.program_id(0)
    pairs = images // 2
    me = lax.axis_index("sp")
    down = kind == "down"
    rows, width, chans = xa_ref.shape[1:]
    out_chans = z_ref.shape[3]
    ways = ((0, me > 0, me < n - 1, me + 1), (1, me < n - 1, me > 0, me - 1))
    if down:
        ways = ((0, me < n - 1, me > 0, me - 1),)

    def coef():
        return coefficients(tot_in, bn_ref, count) if normalize else None

    def start_sends(pair):
        for way, _, sends, peer in ways:
            @pl.when(sends)
            def _():
                for k in range(2):
                    halo_copy(sbuf, halo, hs_sem, hr_sem, way, 2 * pair + k, peer).start()

    def wait_halo(image):
        for way, receives, _, peer in ways:
            @pl.when(receives)
            def _():
                halo_copy(sbuf, halo, hs_sem, hr_sem, way, image, peer).wait_recv()

    def edge_rows(pair):
        c = coef()
        if down:
            for k in range(2):
                even, odd = split_columns(normed(edge_refs[0][k, 0], c), lanes, rows + k)
                sbuf[0, 2 * pair + k, 0] = even.astype(BF)
                sbuf[0, 2 * pair + k, 1] = odd.astype(BF)
            return
        sbuf[1, pl.ds(2 * pair, 2)] = normed(edge_refs[0][:, 0], None if c is None else [v[None] for v in c]).astype(BF)
        sbuf[0, pl.ds(2 * pair, 2)] = normed(edge_refs[1][:, 0], None if c is None else [v[None] for v in c]).astype(BF)

    def prep(image, x_ref, buf):
        c = coef()
        if down:
            for r in range(rows):
                even, odd = split_columns(normed(x_ref[0, r], c), lanes, r)
                buf[r, :, 0:chans] = even.astype(BF)
                buf[r, :, chans : 2 * chans] = odd.astype(BF)
                buf[r, :, 2 * chans :] = shifted(even)[1]
            even = halo[0, image, 0]
            buf[rows, :, 0:chans] = even
            buf[rows, :, chans : 2 * chans] = halo[0, image, 1]
            buf[rows, :, 2 * chans :] = shifted(even.astype(F32))[1]
            return
        for r in range(rows):
            hf = normed(x_ref[0, r], c)
            left, right = shifted(hf)
            buf[r + 1, :, 0:chans] = left
            buf[r + 1, :, chans : 2 * chans] = hf.astype(BF)
            buf[r + 1, :, 2 * chans :] = right
        for way, r in ((0, 0), (1, rows + 1)):
            h = halo[way, image]
            left, right = shifted(h.astype(F32))
            buf[r, :, 0:chans] = left
            buf[r, :, chans : 2 * chans] = h
            buf[r, :, 2 * chans :] = right

    def multiply(k, buf):
        out_rows = z_ref.shape[1]
        step = 2 if down else 1
        if kind == "a":
            for r in range(out_rows):
                lhs = jnp.concatenate([buf[r], buf[r + 1], buf[r + 2]], axis=1)
                z = jnp.dot(lhs, w_ref[...], preferred_element_type=F32)
                z_ref[k, r] = z
                add_sums(st, z, slice(0, out_chans))
            return
        lhs = jnp.concatenate(
            [jnp.concatenate([buf[step * r + dy] for r in range(out_rows)], axis=0) for dy in range(3)], axis=1
        )
        for first in range(0, out_chans, 2 * TILE):
            cols = slice(first, first + 2 * TILE)
            z = jnp.dot(lhs, w_ref[:, cols], preferred_element_type=F32)
            for r in range(out_rows):
                z_ref[k, r, :, cols] = z[r * z_ref.shape[2] : (r + 1) * z_ref.shape[2]]
            add_sums(st, z, cols)

    @pl.when(t == 0)
    def _():
        greet(n)
        st[...] = jnp.zeros_like(st)
        for way, receives, _, _ in ways:
            @pl.when(jnp.logical_not(receives))
            def _():
                halo[way] = jnp.zeros(halo.shape[1:], BF)

    @pl.when(jnp.logical_and(t >= 1, t <= pairs))
    def _():
        start_sends(t - 1)

    @pl.when(t < LEAD)
    def _():
        edge_rows(t)

    @pl.when(t == LEAD - 1)
    def _():
        wait_halo(0)
        prep(0, xb_ref, bufs[0])

    @pl.when(t >= LEAD)
    def _():
        pair = t - LEAD
        after = jnp.minimum(2 * pair + 2, images - 1)
        wait_halo(2 * pair + 1)

        @pl.when(pair < pairs - 1)
        def _():
            wait_halo(2 * pair + 2)

        multiply(0, bufs[0])
        prep(2 * pair + 1, xa_ref, bufs[1])
        multiply(1, bufs[1])
        prep(after, xb_ref, bufs[0])
        edge_rows(jnp.minimum(t, pairs))

    @pl.when(t == pairs + LEAD - 1)
    def _():
        for way, _, sends, peer in ways:
            @pl.when(sends)
            def _():
                @pl.loop(0, images)
                def _(image):
                    halo_copy(sbuf, halo, hs_sem, hr_sem, way, image, peer).wait_send()

        exchange_sums(n, st, own, slots, ss_sem, sr_sem, tot_ref)


def sum_scratch(n, chans):
    return [pltpu.VMEM((2, 8, chans), F32), pltpu.VMEM((8, chans), F32), pltpu.VMEM((n - 1, 8, chans), F32)]


def conv_layer(n, kind, collective_id, x, moments, w):
    images, rows, width, chans = x.shape
    out_chans = w.shape[-1]
    down = kind == "down"
    out_rows, out_width = (rows // 2, width // 2) if down else (rows, width)
    pairs = images // 2
    last = images - 1
    whole = lambda a: pl.BlockSpec(a.shape, lambda t: (0,) * a.ndim, pipeline_mode=pl.Buffered(1))
    edge = lambda row: pl.BlockSpec((2, 1, width, chans), lambda t: (jnp.minimum(t, pairs - 1), row, 0, 0))
    w2 = w.reshape(9 * chans, out_chans)
    in_specs = [
        pl.BlockSpec((1, rows, width, chans), lambda t: (jnp.clip(2 * (t - LEAD) + 1, 1, last), 0, 0, 0)),
        pl.BlockSpec((1, rows, width, chans), lambda t: (jnp.clip(2 * (t - LEAD) + 2, 0, last), 0, 0, 0)),
        edge(0),
    ] + ([] if down else [edge(rows - 1)])
    args = [x] * len(in_specs)
    count = 1.0
    if moments is not None:
        tot, bn = moments
        count = float(images * rows * width * n)
        in_specs += [whole(tot), whole(bn)]
        args += [tot, bn]
    in_specs.append(whole(w2))
    args.append(w2)
    n_ways = 1 if down else 2
    message = (2, width // 2, chans) if down else (width, chans)
    buf = pltpu.VMEM((rows + 1, width // 2, 3 * chans) if down else (rows + 2, width, 3 * chans), BF)
    pixels = images * out_rows * out_width
    return pl.pallas_call(
        functools.partial(conv_kernel, n, images, kind, moments is not None, count),
        grid=(pairs + LEAD,),
        in_specs=in_specs,
        out_specs=[
            pl.BlockSpec((2, out_rows, out_width, out_chans), lambda t: (jnp.maximum(t - LEAD, 0), 0, 0, 0)),
            pl.BlockSpec((8, out_chans), lambda t: (0, 0)),
        ],
        out_shape=[
            jax.ShapeDtypeStruct((images, out_rows, out_width, out_chans), F32),
            jax.ShapeDtypeStruct((8, out_chans), F32),
        ],
        scratch_shapes=[
            buf,
            buf,
            pltpu.VMEM((n_ways, images + 2) + message, BF),
            pltpu.VMEM((n_ways, images) + message, BF),
            *sum_scratch(n, out_chans),
            pltpu.SemaphoreType.DMA((n_ways, images)),
            pltpu.SemaphoreType.DMA((n_ways, images)),
            pltpu.SemaphoreType.DMA((n - 1,)),
            pltpu.SemaphoreType.DMA((n - 1,)),
        ]
        + ([pltpu.VMEM((rows + 2, chans // 128, width, 128), F32)] if down else []),
        compiler_params=pltpu.CompilerParams(collective_id=collective_id, has_side_effects=True, vmem_limit_bytes=VMEM),
        cost_estimate=pl.CostEstimate(flops=2 * pixels * 9 * chans * out_chans, bytes_accessed=x.nbytes + pixels * out_chans * 4, transcendentals=0),
        name=f"conv_{kind}",
    )(*args)


def dot_tiles(lhs_ref, w_ref, emit):
    for r in range(2):
        for first in range(0, w_ref.shape[1], 2 * TILE):
            cols = slice(first, first + 2 * TILE)
            emit(r, cols, jnp.dot(lhs_ref[0, r], w_ref[:, cols], preferred_element_type=F32))


def around(n, st, own, slots, ss_sem, sr_sem, tot_ref, images, work):
    s = pl.program_id(0)

    @pl.when(s == 0)
    def _():
        greet(n)
        st[...] = jnp.zeros_like(st)

    work()

    @pl.when(s == images - 1)
    def _():
        exchange_sums(n, st, own, slots, ss_sem, sr_sem, tot_ref)


def enter_kernel(n, images, count, x_ref, tot_in, bn_ref, w_ref, h_ref, z_ref, tot_ref, st, own, slots, ss_sem, sr_sem):
    def work():
        c = coefficients(tot_in, bn_ref, count)
        for r in range(2):
            h_ref[0, r] = normed(x_ref[0, r], c).astype(BF)

        def emit(r, cols, z):
            z_ref[0, r, :, cols] = z
            add_sums(st, z, cols)

        dot_tiles(h_ref, w_ref, emit)

    around(n, st, own, slots, ss_sem, sr_sem, tot_ref, images, work)


def sums_kernel(n, images, count, x_ref, tot_in, bn_ref, w_ref, u_ref, tot_ref, st, own, slots, ss_sem, sr_sem):
    def work():
        c = coefficients(tot_in, bn_ref, count)
        for r in range(2):
            u_ref[0, r] = normed(x_ref[0, r], c).astype(BF)
        dot_tiles(u_ref, w_ref, lambda r, cols, z: add_sums(st, z, cols))

    around(n, st, own, slots, ss_sem, sr_sem, tot_ref, images, work)


def leave(u_ref, h_ref, tot_in, bn_ref, w_ref, o_ref, count):
    mean, scale, shift = coefficients(tot_in, bn_ref, count)

    def emit(r, cols, z):
        y = (z - mean[:, cols]) * scale[:, cols] + shift[:, cols] + h_ref[0, r, :, cols].astype(F32)
        o_ref[0, r, :, cols] = jnp.maximum(y, 0.0).astype(BF)

    dot_tiles(u_ref, w_ref, emit)


def leave_enter_kernel(n, images, count, u_ref, h_ref, tot_in, bn_ref, w_ref, w_next, o_ref, z_ref, tot_ref, st, own, slots, ss_sem, sr_sem):
    def work():
        leave(u_ref, h_ref, tot_in, bn_ref, w_ref, o_ref, count)

        def emit(r, cols, z):
            z_ref[0, r, :, cols] = z
            add_sums(st, z, cols)

        dot_tiles(o_ref, w_next, emit)

    around(n, st, own, slots, ss_sem, sr_sem, tot_ref, images, work)


def leave_kernel(count, u_ref, h_ref, tot_in, bn_ref, w_ref, o_ref):
    leave(u_ref, h_ref, tot_in, bn_ref, w_ref, o_ref, count)


def point_call(n, kernel, collective_id, name, blocked, fixed, outs, sums, flops):
    images, rows, width = blocked[0].shape[:3]
    count = float(images * rows * width * n)
    block = lambda c: pl.BlockSpec((1, rows, width, c), lambda s: (s, 0, 0, 0))
    whole = lambda a: pl.BlockSpec(a.shape, lambda s: (0,) * a.ndim, pipeline_mode=pl.Buffered(1))
    out_specs = [block(c) for c, _ in outs]
    out_shape = [jax.ShapeDtypeStruct((images, rows, width, c), d) for c, d in outs]
    scratch = []
    if sums:
        out_specs.append(pl.BlockSpec((8, sums), lambda s: (0, 0)))
        out_shape.append(jax.ShapeDtypeStruct((8, sums), F32))
        scratch = [*sum_scratch(n, sums), pltpu.SemaphoreType.DMA((n - 1,)), pltpu.SemaphoreType.DMA((n - 1,))]
        kernel = functools.partial(kernel, n, images, count)
        params = pltpu.CompilerParams(collective_id=collective_id, has_side_effects=True, vmem_limit_bytes=VMEM)
    else:
        kernel = functools.partial(kernel, count)
        params = pltpu.CompilerParams(vmem_limit_bytes=VMEM)
    return pl.pallas_call(
        kernel,
        grid=(images,),
        in_specs=[block(a.shape[3]) for a in blocked] + [whole(a) for a in fixed],
        out_specs=out_specs,
        out_shape=out_shape,
        scratch_shapes=scratch,
        compiler_params=params,
        cost_estimate=pl.CostEstimate(flops=flops, bytes_accessed=sum(a.nbytes for a in blocked), transcendentals=0),
        name=name,
    )(*blocked, *fixed)


def solution(mesh):
    n = mesh.shape["sp"]

    def forward(images, w_a, bn_a, w_down, bn_down, w_in, bn_in, w_mid, bn_mid, w_out, bn_out):
        z, tot = conv_layer(n, "a", 0, images, None, w_a[0])
        for layer in range(1, w_a.shape[0]):
            z, tot = conv_layer(n, "a", 1, z, (tot, bn_a[layer - 1]), w_a[layer])
        z, tot = conv_layer(n, "down", 2, z, (tot, bn_a[w_a.shape[0] - 1]), w_down)
        wide, slim = w_down.shape[-1], w_in.shape[-1]
        pixels = z.shape[0] * z.shape[1] * z.shape[2]
        flops = 2 * pixels * wide * slim
        hidden, z, tot = point_call(n, enter_kernel, 3, "enter", [z], [tot, bn_down, w_in[0]], [(wide, BF), (slim, F32)], slim, flops)
        blocks = w_in.shape[0]
        for block in range(blocks):
            z, tot = conv_layer(n, "mid", 4, z, (tot, bn_in[block]), w_mid[block])
            branch, tot = point_call(n, sums_kernel, 5, "sums", [z], [tot, bn_mid[block], w_out[block]], [(slim, BF)], wide, flops)
            fixed = [tot, bn_out[block], w_out[block]]
            if block + 1 < blocks:
                hidden, z, tot = point_call(n, leave_enter_kernel, 6, "leave_enter", [branch, hidden], fixed + [w_in[block + 1]], [(wide, BF), (slim, F32)], slim, 2 * flops)
            else:
                hidden = point_call(n, leave_kernel, None, "leave", [branch, hidden], fixed, [(wide, BF)], 0, flops)[0]
        return hidden

    act_spec = P("dp", "sp", None, None)
    return jax.shard_map(forward, mesh=mesh, in_specs=(act_spec,) + (P(),) * 10, out_specs=act_spec, check_vma=False)
```

time: 1390 us -> 748 us (0.54)
  Pallas kernels: 0 us -> 715 us
  matrix products: 642 us -> 0 us
  blocking collectives: 364 us -> 0 us
  other arithmetic: 231 us -> 0 us
  waiting for transfers between devices: 53.7 us -> 0 us
  local copies, waits for them, and re-layouts: 64.8 us -> 24.7 us
  starting transfers between devices: 21.9 us -> 0 us
    pallas_call x0 -> x12, Pallas kernels: none -> 715 us  [the longest x7 512 us: conv_layer(): pl.pallas_call(functools.partial(conv_kernel, n, images, kind, moments is...]
    conv_general_dilated x7 -> x0, matrix products: 436 us -> none  [the longest x6 348 us: conv_same(): lax.conv_general_dilated(padded, weight, (1, 1), ((0, 0), (1, 1)), dimens...]
    psum x11 -> x0, blocking collectives: 364 us -> none  [batch_norm(): group_moments = lax.psum(part_sums, 'sp') / norm_count]
    convert_element_type x9 -> x0, other arithmetic: 227 us -> none  [the longest x2 124 us: forward(): hidden = jax.nn.relu(summed).astype(jnp.bfloat16)]
    dot_general x4 -> x0, matrix products: 206 us -> none  [conv_point(): jnp.einsum('bhwc,cd->bhwd', hidden, weight, preferred_element_type=jnp.fl...]
    ppermute x13 -> x0, waiting for transfers between devices: 53.7 us -> none  [the longest x6 24.3 us: conv_same(): from_below = lax.ppermute(hidden[:, :1], 'sp', to_prev)]
    convert_element_type x1 -> x0, local copies, waits for them, and re-layouts: 30.2 us -> none  [forward(): hidden = jax.nn.relu(summed).astype(jnp.bfloat16)]
    ppermute x13 -> x0, starting transfers between devices: 21.9 us -> none  [the longest x6 12.3 us: conv_same(): from_above = lax.ppermute(hidden[:, -1:], 'sp', to_next)]
  transfers between devices with their start and end apart: 13 -> 0, of which waited for: 13 -> 0; matrix products, arithmetic and copies ran while one was open for 1% -> 0% of each run, Pallas kernels for 0% -> 0%
where the time goes in v1:
time: 748 us; the launch traced here: 740 us
  Pallas kernels  715 us (96%)
  local copies, waits for them, and re-layouts  24.7 us (3%)
    pallas_call x7, Pallas kernels, conv_layer(): pl.pallas_call(functools.partial(conv_kernel, n, images, kind, moments is...  512 us
    pallas_call x5, Pallas kernels, point_call(): pl.pallas_call(kernel, grid=(images,), in_specs=[block(a.shape[3]) for a...  202 us

profile of v1, /device:TPU:0, one launch (start us, length us, event | category | flops | bytes accessed | tf_op | source)
XLA Modules:
  0.0 740.3 jit_solution(3897885550262327030)
XLA Ops:
  0.0 4.6 fusion.1
  4.6 0.0 copy-start.1
  4.6 65.8 %conv_a.4 = (f32[16,4,512,256]{3,2,1,0:T(8,128)}, f32[8,256]{1,0:T(8,128)}) custom-call(bf16[16,4,512,256]{3,2,1,0:T(8,128)(2,1)} %refs_3_.1, bf16[16,4,512,256]{3,2,1,0:T(8,128)(2,1)} %refs_3_.1, bf16[16,4,512,256]{3,2,1,0:T(8,128)(2,1)} %refs_3_.1, bf16[16,4,512,256]{3,2,1,0:T(8,128)(2,1)} %refs_3_.1, bf16[2304,256]{1,0:T(8,128)(2,1)} %bitcast.40), custom_call_target="tpu_custom_call" | custom-call | flops 38654705664 | bytes 50331648 | tf_op jit(solution)/shard_map/conv_a/pallas_call | solution.py:277
  70.4 0.0 copy-done.1
  70.4 0.6 slice_bitcast_fusion.10
  71.0 67.3 %conv_a.5 = (f32[16,4,512,256]{3,2,1,0:T(8,128)}, f32[8,256]{1,0:T(8,128)}) custom-call(f32[16,4,512,256]{3,2,1,0:T(8,128)} %get-tuple-element.29.refs_0_.refs_1_.refs_2_.refs_3_, f32[16,4,512,256]{3,2,1,0:T(8,128)} %get-tuple-element.29.refs_0_.refs_1_.refs_2_.refs_3_, f32[16,4,512,256]{3,2,1,0:T(8,128)} %get-tuple-element.29.refs_0_.refs_1_.refs_2_.refs_3_, ...), custom_call_target="tpu_custom_call" | custom-call | flops 38654705664 | bytes 67108864 | tf_op jit(solution)/shard_map/conv_a/pallas_call | solution.py:277
  138.3 68.3 %conv_a.6 = (f32[16,4,512,256]{3,2,1,0:T(8,128)}, f32[8,256]{1,0:T(8,128)}) custom-call(f32[16,4,512,256]{3,2,1,0:T(8,128)} %get-tuple-element.31.refs_0_.refs_1_.refs_2_.refs_3_, f32[16,4,512,256]{3,2,1,0:T(8,128)} %get-tuple-element.31.refs_0_.refs_1_.refs_2_.refs_3_, f32[16,4,512,256]{3,2,1,0:T(8,128)} %get-tuple-element.31.refs_0_.refs_1_.refs_2_.refs_3_, ...), custom_call_target="tpu_custom_call" | custom-call | flops 38654705664 | bytes 67108864 | tf_op jit(solution)/shard_map/conv_a/pallas_call | solution.py:277
  206.6 67.5 %conv_a.7 = (f32[16,4,512,256]{3,2,1,0:T(8,128)}, f32[8,256]{1,0:T(8,128)}) custom-call(f32[16,4,512,256]{3,2,1,0:T(8,128)} %get-tuple-element.33.refs_0_.refs_1_.refs_2_.refs_3_, f32[16,4,512,256]{3,2,1,0:T(8,128)} %get-tuple-element.33.refs_0_.refs_1_.refs_2_.refs_3_, f32[16,4,512,256]{3,2,1,0:T(8,128)} %get-tuple-element.33.refs_0_.refs_1_.refs_2_.refs_3_, ...), custom_call_target="tpu_custom_call" | custom-call | flops 38654705664 | bytes 67108864 | tf_op jit(solution)/shard_map/conv_a/pallas_call | solution.py:277
  274.1 109.7 %conv_down.1 = (f32[16,2,256,2048]{3,2,1,0:T(8,128)}, f32[8,2048]{1,0:T(8,128)}) custom-call(f32[16,4,512,256]{3,2,1,0:T(8,128)} %get-tuple-element.35.refs_0_.refs_1_.refs_2_, f32[16,4,512,256]{3,2,1,0:T(8,128)} %get-tuple-element.35.refs_0_.refs_1_.refs_2_, f32[16,4,512,256]{3,2,1,0:T(8,128)} %get-tuple-element.35.refs_0_.refs_1_.refs_2_, ...), custom_call_target="tpu_custom_call" | custom-call | flops 77309411328 | bytes 100663296 | tf_op jit(solution)/shard_map/conv_down/pallas_call | solution.py:277
  383.9 4.5 slice_bitcast_fusion.1
  388.4 52.6 %enter.1 = (bf16[16,2,256,2048]{3,2,1,0:T(8,128)(2,1)}, f32[16,2,256,512]{3,2,1,0:T(8,128)}, f32[8,512]{1,0:T(8,128)}) custom-call(f32[16,2,256,2048]{3,2,1,0:T(8,128)} %get-tuple-element.37.x_ref, f32[8,2048]{1,0:T(8,128)} %get-tuple-element.38.tot_in, f32[2,2048]{1,0:T(2,128)} %bn_ref.1, bf16[2048,512]{1,0:T(8,128)(2,1)} %get-tuple-element.62.w_ref), custom_call_target="tpu_custom_call" | custom-call | flops 17179869184 | bytes 67108864 | tf_op jit(solution)/shard_map/enter/pallas_call | solution.py:398
  441.0 0.0 copy-start.2
  441.1 8.3 %fusion = (bf16[1,3,3,512,512]{4,3,2,1,0:T(8,128)(2,1)}, bf16[1,3,3,512,512]{4,3,2,1,0:T(8,128)(2,1)}) fusion(bf16[2,3,3,512,512]{4,3,2,1,0:T(8,128)(2,1)} %param.18), kind=kLoop, calls=%fused_computation.14 | loop fusion | bytes 18874368 | tf_op jit(solution)/shard_map/slice | solution.py:425
  449.3 0.0 copy-done.2
  449.3 0.6 slice_bitcast_fusion.7
  449.9 67.5 %conv_mid.2 = (f32[16,2,256,512]{3,2,1,0:T(8,128)}, f32[8,512]{1,0:T(8,128)}) custom-call(f32[16,2,256,512]{3,2,1,0:T(8,128)} %get-tuple-element.39.refs_0_.refs_1_.refs_2_.refs_3_, f32[16,2,256,512]{3,2,1,0:T(8,128)} %get-tuple-element.39.refs_0_.refs_1_.refs_2_.refs_3_, f32[16,2,256,512]{3,2,1,0:T(8,128)} %get-tuple-element.39.refs_0_.refs_1_.refs_2_.refs_3_, ...), custom_call_target="tpu_custom_call" | custom-call | flops 38654705664 | bytes 33554432 | tf_op jit(solution)/shard_map/conv_mid/pallas_call | solution.py:277
  517.5 0.0 copy-start.3
  517.5 4.9 slice_bitcast_fusion
  522.4 0.0 copy-done.3
  522.4 0.6 slice_bitcast_fusion.6
  523.0 0.0 copy-start
  523.0 29.8 %sums.2 = (bf16[16,2,256,512]{3,2,1,0:T(8,128)(2,1)}, f32[8,2048]{1,0:T(8,128)}) custom-call(f32[16,2,256,512]{3,2,1,0:T(8,128)} %get-tuple-element.41.x_ref, f32[8,512]{1,0:T(8,128)} %get-tuple-element.42.tot_in, f32[2,512]{1,0:T(2,128)} %get-tuple-element.66.bn_ref, bf16[512,2048]{1,0:T(8,128)(2,1)} %get-tuple-element.60.w_ref), custom_call_target="tpu_custom_call" | custom-call | flops 17179869184 | bytes 16777216 | tf_op jit(solution)/shard_map/sums/pallas_call | solution.py:398
  552.8 0.0 copy-done
  552.8 0.6 slice_bitcast_fusion.4
  553.4 53.7 %leave_enter.1 = (bf16[16,2,256,2048]{3,2,1,0:T(8,128)(2,1)}, f32[16,2,256,512]{3,2,1,0:T(8,128)}, f32[8,512]{1,0:T(8,128)}) custom-call(bf16[16,2,256,512]{3,2,1,0:T(8,128)(2,1)} %get-tuple-element.43.u_ref, bf16[16,2,256,2048]{3,2,1,0:T(8,128)(2,1)} %get-tuple-element.44.h_ref, f32[8,2048]{1,0:T(8,128)} %get-tuple-element.45.tot_in, ...), custom_call_target="tpu_custom_call" | custom-call | flops 34359738368 | bytes 41943040 | tf_op jit(solution)/shard_map/leave_enter/pallas_call | solution.py:398
  607.2 66.4 %conv_mid.3 = (f32[16,2,256,512]{3,2,1,0:T(8,128)}, f32[8,512]{1,0:T(8,128)}) custom-call(f32[16,2,256,512]{3,2,1,0:T(8,128)} %get-tuple-element.46.refs_0_.refs_1_.refs_2_.refs_3_, f32[16,2,256,512]{3,2,1,0:T(8,128)} %get-tuple-element.46.refs_0_.refs_1_.refs_2_.refs_3_, f32[16,2,256,512]{3,2,1,0:T(8,128)} %get-tuple-element.46.refs_0_.refs_1_.refs_2_.refs_3_, ...), custom_call_target="tpu_custom_call" | custom-call | flops 38654705664 | bytes 33554432 | tf_op jit(solution)/shard_map/conv_mid/pallas_call | solution.py:277
  673.6 29.8 %sums.3 = (bf16[16,2,256,512]{3,2,1,0:T(8,128)(2,1)}, f32[8,2048]{1,0:T(8,128)}) custom-call(f32[16,2,256,512]{3,2,1,0:T(8,128)} %get-tuple-element.48.x_ref, f32[8,512]{1,0:T(8,128)} %get-tuple-element.49.tot_in, f32[2,512]{1,0:T(2,128)} %get-tuple-element.65.bn_ref, bf16[512,2048]{1,0:T(8,128)(2,1)} %get-tuple-element.59.w_ref), custom_call_target="tpu_custom_call" | custom-call | flops 17179869184 | bytes 16777216 | tf_op jit(solution)/shard_map/sums/pallas_call | solution.py:398
  703.4 36.5 %leave.1 = bf16[16,2,256,2048]{3,2,1,0:T(8,128)(2,1)} custom-call(bf16[16,2,256,512]{3,2,1,0:T(8,128)(2,1)} %get-tuple-element.50.u_ref, bf16[16,2,256,2048]{3,2,1,0:T(8,128)(2,1)} %get-tuple-element.51.h_ref, f32[8,2048]{1,0:T(8,128)} %get-tuple-element.52.tot_in, f32[2,2048]{1,0:T(2,128)} %get-tuple-element.63.bn_ref, ...), custom_call_target="tpu_custom_call" | custom-call | flops 17179869184 | bytes 41943040 | tf_op jit(solution)/shard_map/leave/pallas_call | solution.py:398
Async XLA Ops:
  4.6 65.8 %copy-start.1 = (f32[4,2,256]{2,1,0:T(2,128)S(1)}, f32[4,2,256]{2,1,0:T(2,128)}, u32[]{:S(2)}) copy-start(f32[4,2,256]{2,1,0:T(2,128)} %param.13) | copy-start | bytes 24580
  441.0 8.3 %copy-start.2 = (f32[2,2,512]{2,1,0:T(2,128)S(1)}, f32[2,2,512]{2,1,0:T(2,128)}, u32[]{:S(2)}) copy-start(f32[2,2,512]{2,1,0:T(2,128)} %param.17) | copy-start | bytes 24580
  517.5 4.9 copy-start.3
  523.0 29.8 %copy-start = (f32[2,2,2048]{2,1,0:T(2,128)S(1)}, f32[2,2,2048]{2,1,0:T(2,128)}, u32[]{:S(2)}) copy-start(f32[2,2,2048]{2,1,0:T(2,128)} %param.21) | copy-start | bytes 98308

commit v2 on v1

v2 whole, which is shorter than its diff:
```python
import functools
import itertools

import jax
import jax.numpy as jnp
from jax import lax
from jax.experimental import pallas as pl
from jax.experimental.pallas import tpu as pltpu
from jax.sharding import PartitionSpec as P

NORM_EPS = 1e-5
BF, F32 = jnp.bfloat16, jnp.float32
TILE = 256
PER_STEP = {"enter": 2, "sums": 2, "leave_enter": 2, "leave": 2}
LEAD = 3
VMEM = 64000 * 1024


def coefficients(tot_ref, bn_ref, count):
    mean = tot_ref[0:1, :] / count
    var = tot_ref[1:2, :] / count - mean * mean
    return mean, bn_ref[0:1, :] * lax.rsqrt(var + NORM_EPS), bn_ref[1:2, :]


def normed(z, coef):
    if coef is None:
        return z.astype(F32)
    mean, scale, shift = coef
    return jnp.maximum((z - mean) * scale + shift, 0.0)


def column_sums(z):
    z3 = z.reshape(z.shape[0] // 8, 8, z.shape[1])
    return jnp.sum(z3, axis=0), jnp.sum(z3 * z3, axis=0)


def add_sums(st_ref, z, cols):
    first, second = column_sums(z)
    st_ref[0, :, cols] += first
    st_ref[1, :, cols] += second


def greet(n):
    me = lax.axis_index("sp")
    for d in range(1, n):
        pl.semaphore_signal(
            pltpu.get_barrier_semaphore(), 1, device_id={"sp": lax.rem(me + d, n)}, device_id_type=pl.DeviceIdType.MESH
        )


def await_greetings(n):
    pl.semaphore_wait(pltpu.get_barrier_semaphore(), n - 1)


def sum_copies(n, own, slots, send_sem, recv_sem):
    me = lax.axis_index("sp")
    return [
        pltpu.make_async_remote_copy(
            src_ref=own,
            dst_ref=slots.at[d - 1],
            send_sem=send_sem.at[d - 1],
            recv_sem=recv_sem.at[d - 1],
            device_id={"sp": lax.rem(me + d, n)},
            device_id_type=pl.DeviceIdType.MESH,
        )
        for d in range(1, n)
    ]


def send_sums(n, st_ref, own, slots, send_sem, recv_sem):
    own[0:1, :] = jnp.sum(st_ref[0], axis=0, keepdims=True)
    own[1:2, :] = jnp.sum(st_ref[1], axis=0, keepdims=True)
    for copy in sum_copies(n, own, slots, send_sem, recv_sem):
        copy.start()


def receive_sums(n, own, slots, send_sem, recv_sem, tot_ref):
    for copy in sum_copies(n, own, slots, send_sem, recv_sem):
        copy.wait()
    total = own[...]
    for d in range(n - 1):
        total = total + slots[d]
    tot_ref[...] = total


def shifted(hf):
    width = hf.shape[0]
    col = lax.broadcasted_iota(jnp.int32, hf.shape, 0)
    left = jnp.where(col == 0, 0.0, pltpu.roll(hf, 1, 0)).astype(BF)
    right = jnp.where(col == width - 1, 0.0, pltpu.roll(hf, width - 1, 0)).astype(BF)
    return left, right


def split_columns(hf, lanes, slot):
    width, chans = hf.shape
    for half in range(chans // 128):
        lanes[slot, half] = hf[:, half * 128 : (half + 1) * 128]
    return [
        jnp.concatenate([lanes[slot, half, pl.ds(parity, width // 2, stride=2), :] for half in range(chans // 128)], axis=1)
        for parity in range(2)
    ]


def halo_copy(sbuf, halo, send_sem, recv_sem, way, image, peer):
    return pltpu.make_async_remote_copy(
        src_ref=sbuf.at[way, image],
        dst_ref=halo.at[way, image],
        send_sem=send_sem.at[way, image],
        recv_sem=recv_sem.at[way, image],
        device_id={"sp": peer},
        device_id_type=pl.DeviceIdType.MESH,
    )


def conv_kernel(n, images, kind, layer, normalize, count, *refs):
    refs = list(refs)
    xa_ref, xb_ref = refs.pop(0), refs.pop(0)
    edge_refs = [refs.pop(0) for _ in range(1 if kind == "down" else 2)]
    tot_in, bn_ref = (refs.pop(0), refs.pop(0)) if normalize else (None, None)
    w_hbm, z_ref, tot_ref, w_ref, w_sem, buf0, buf1, sbuf, halo, st, own, slots, hs_sem, hr_sem, ss_sem, sr_sem, *rest = refs
    lanes = rest[0] if rest else None
    bufs = (buf0, buf1)
    t = pl.program_id(0)
    pairs = images // 2
    me = lax.axis_index("sp")
    down = kind == "down"
    rows, width, chans = xa_ref.shape[1:]
    out_chans = z_ref.shape[3]
    ways = ((0, me > 0, me < n - 1, me + 1), (1, me < n - 1, me > 0, me - 1))
    if down:
        ways = ((0, me < n - 1, me > 0, me - 1),)

    def coef():
        return coefficients(tot_in, bn_ref, count) if normalize else None

    def start_sends(pair):
        for way, _, sends, peer in ways:
            @pl.when(sends)
            def _():
                for k in range(2):
                    halo_copy(sbuf, halo, hs_sem, hr_sem, way, 2 * pair + k, peer).start()

    def wait_halo(image):
        for way, receives, _, peer in ways:
            @pl.when(receives)
            def _():
                halo_copy(sbuf, halo, hs_sem, hr_sem, way, image, peer).wait_recv()

    def edge_rows(pair):
        c = coef()
        if down:
            for k in range(2):
                even, odd = split_columns(normed(edge_refs[0][k, 0], c), lanes, rows + k)
                sbuf[0, 2 * pair + k, 0] = even.astype(BF)
                sbuf[0, 2 * pair + k, 1] = odd.astype(BF)
            return
        sbuf[1, pl.ds(2 * pair, 2)] = normed(edge_refs[0][:, 0], None if c is None else [v[None] for v in c]).astype(BF)
        sbuf[0, pl.ds(2 * pair, 2)] = normed(edge_refs[1][:, 0], None if c is None else [v[None] for v in c]).astype(BF)

    def prep_own(x_ref, buf):
        c = coef()
        if down:
            for r in range(rows):
                even, odd = split_columns(normed(x_ref[0, r], c), lanes, r)
                buf[r, :, 0:chans] = even.astype(BF)
                buf[r, :, chans : 2 * chans] = odd.astype(BF)
                buf[r, :, 2 * chans :] = shifted(even)[1]
            return
        for r in range(rows):
            hf = normed(x_ref[0, r], c)
            left, right = shifted(hf)
            buf[r + 1, :, 0:chans] = left
            buf[r + 1, :, chans : 2 * chans] = hf.astype(BF)
            buf[r + 1, :, 2 * chans :] = right

    def prep_halo(image, buf):
        if down:
            even = halo[0, image, 0]
            buf[rows, :, 0:chans] = even
            buf[rows, :, chans : 2 * chans] = halo[0, image, 1]
            buf[rows, :, 2 * chans :] = shifted(even.astype(F32))[1]
            return
        for way, r in ((0, 0), (1, rows + 1)):
            h = halo[way, image]
            left, right = shifted(h.astype(F32))
            buf[r, :, 0:chans] = left
            buf[r, :, chans : 2 * chans] = h
            buf[r, :, 2 * chans :] = right

    def multiply(k, buf):
        out_rows = z_ref.shape[1]
        if kind == "a":
            for r in range(out_rows):
                lhs = jnp.concatenate([buf[r], buf[r + 1], buf[r + 2]], axis=1)
                z = jnp.dot(lhs, w_ref[...], preferred_element_type=F32)
                z_ref[k, r] = z
                add_sums(st, z, slice(0, out_chans))
            return
        step = 2 if down else 1
        lhs = jnp.concatenate(
            [jnp.concatenate([buf[step * r + dy] for r in range(out_rows)], axis=0) for dy in range(3)], axis=1
        )
        for first in range(0, out_chans, 2 * TILE):
            cols = slice(first, first + 2 * TILE)
            z = jnp.dot(lhs, w_ref[:, cols], preferred_element_type=F32)
            for r in range(out_rows):
                z_ref[k, r, :, cols] = z[r * z_ref.shape[2] : (r + 1) * z_ref.shape[2]]
            add_sums(st, z, cols)

    load_weights = pltpu.make_async_copy(w_hbm.at[layer], w_ref, w_sem)

    @pl.when(t == 0)
    def _():
        load_weights.start()
        greet(n)
        st[...] = jnp.zeros_like(st)
        edge_rows(0)
        await_greetings(n)
        start_sends(0)

    @pl.when(jnp.logical_and(t >= 2, t <= pairs))
    def _():
        start_sends(t - 1)

    @pl.when(t == 1)
    def _():
        for way, receives, _, _ in ways:
            @pl.when(jnp.logical_not(receives))
            def _():
                halo[way] = jnp.zeros(halo.shape[1:], BF)

    @pl.when(jnp.logical_and(t >= 1, t < LEAD))
    def _():
        edge_rows(t)

    @pl.when(t == LEAD - 1)
    def _():
        prep_own(xb_ref, bufs[0])
        load_weights.wait()

    @pl.when(t >= LEAD)
    def _():
        pair = t - LEAD
        wait_halo(2 * pair)
        wait_halo(2 * pair + 1)
        prep_halo(2 * pair, bufs[0])
        multiply(0, bufs[0])
        prep_own(xa_ref, bufs[1])
        prep_halo(2 * pair + 1, bufs[1])
        multiply(1, bufs[1])
        prep_own(xb_ref, bufs[0])
        edge_rows(jnp.minimum(t, pairs))

    @pl.when(t == pairs + LEAD - 1)
    def _():
        send_sums(n, st, own, slots, ss_sem, sr_sem)
        for way, _, sends, peer in ways:
            @pl.when(sends)
            def _():
                @pl.loop(0, images)
                def _(image):
                    halo_copy(sbuf, halo, hs_sem, hr_sem, way, image, peer).wait_send()

        receive_sums(n, own, slots, ss_sem, sr_sem, tot_ref)


def sum_scratch(n, chans):
    return [pltpu.VMEM((2, 8, chans), F32), pltpu.VMEM((2, chans), F32), pltpu.VMEM((n - 1, 2, chans), F32)]


def layer_spec(stacked):
    array, layer = stacked
    return pl.BlockSpec((None,) + array.shape[1:], lambda *_: (layer, 0, 0), pipeline_mode=pl.Buffered(1))


def conv_layer(n, kind, layer, collective_id, x, moments, w):
    images, rows, width, chans = x.shape
    out_chans = w.shape[-1]
    down = kind == "down"
    out_rows, out_width = (rows // 2, width // 2) if down else (rows, width)
    pairs = images // 2
    last = images - 1
    whole = lambda a: pl.BlockSpec(a.shape, lambda t: (0,) * a.ndim, pipeline_mode=pl.Buffered(1))
    edge = lambda row: pl.BlockSpec((2, 1, width, chans), lambda t: (jnp.minimum(t, pairs - 1), row, 0, 0))
    w2 = w.reshape(-1, 9 * chans, out_chans)
    in_specs = [
        pl.BlockSpec((1, rows, width, chans), lambda t: (jnp.clip(2 * (t - LEAD) + 1, 1, last), 0, 0, 0)),
        pl.BlockSpec((1, rows, width, chans), lambda t: (jnp.clip(2 * (t - LEAD) + 2, 0, last), 0, 0, 0)),
        edge(0),
    ] + ([] if down else [edge(rows - 1)])
    args = [x] * len(in_specs)
    count = 1.0
    if moments is not None:
        tot, bn = moments
        count = float(images * rows * width * n)
        in_specs += [whole(tot), layer_spec(bn)]
        args += [tot, bn[0]]
    in_specs.append(pl.BlockSpec(memory_space=pl.ANY))
    args.append(w2)
    n_ways = 1 if down else 2
    message = (2, width // 2, chans) if down else (width, chans)
    buf = pltpu.VMEM((rows + 1, width // 2, 3 * chans) if down else (rows + 2, width, 3 * chans), BF)
    pixels = images * out_rows * out_width
    return pl.pallas_call(
        functools.partial(conv_kernel, n, images, kind, layer, moments is not None, count),
        grid=(pairs + LEAD,),
        in_specs=in_specs,
        out_specs=[
            pl.BlockSpec((2, out_rows, out_width, out_chans), lambda t: (jnp.maximum(t - LEAD, 0), 0, 0, 0)),
            pl.BlockSpec((2, out_chans), lambda t: (0, 0)),
        ],
        out_shape=[
            jax.ShapeDtypeStruct((images, out_rows, out_width, out_chans), F32),
            jax.ShapeDtypeStruct((2, out_chans), F32),
        ],
        scratch_shapes=[
            pltpu.VMEM(w2.shape[1:], BF),
            pltpu.SemaphoreType.DMA,
            buf,
            buf,
            pltpu.VMEM((n_ways, images + 2) + message, BF),
            pltpu.VMEM((n_ways, images) + message, BF),
            *sum_scratch(n, out_chans),
            pltpu.SemaphoreType.DMA((n_ways, images)),
            pltpu.SemaphoreType.DMA((n_ways, images)),
            pltpu.SemaphoreType.DMA((n - 1,)),
            pltpu.SemaphoreType.DMA((n - 1,)),
        ]
        + ([pltpu.VMEM((rows + 2, chans // 128, width, 128), F32)] if down else []),
        compiler_params=pltpu.CompilerParams(collective_id=collective_id, has_side_effects=True, vmem_limit_bytes=VMEM),
        cost_estimate=pl.CostEstimate(flops=2 * pixels * 9 * chans * out_chans, bytes_accessed=x.nbytes + pixels * out_chans * 4, transcendentals=0),
        name=f"conv_{kind}",
    )(*args)


def dot_tiles(lhs_ref, w_ref, emit):
    lhs = lhs_ref[...].reshape(-1, lhs_ref.shape[3])
    for first in range(0, w_ref.shape[1], 2 * TILE):
        cols = slice(first, first + 2 * TILE)
        emit(cols, jnp.dot(lhs, w_ref[:, cols], preferred_element_type=F32))


def around(n, st, own, slots, ss_sem, sr_sem, tot_ref, work):
    s = pl.program_id(0)

    @pl.when(s == 0)
    def _():
        greet(n)
        st[...] = jnp.zeros_like(st)

    work()

    @pl.when(s == pl.num_programs(0) - 1)
    def _():
        await_greetings(n)
        send_sums(n, st, own, slots, ss_sem, sr_sem)
        receive_sums(n, own, slots, ss_sem, sr_sem, tot_ref)


def enter_kernel(n, count, x_ref, tot_in, bn_ref, w_ref, h_ref, z_ref, tot_ref, st, own, slots, ss_sem, sr_sem):
    def work():
        c = coefficients(tot_in, bn_ref, count)
        for k in range(x_ref.shape[0]):
            for r in range(x_ref.shape[1]):
                h_ref[k, r] = normed(x_ref[k, r], c).astype(BF)

        def emit(cols, z):
            z_ref[:, :, :, cols] = z.reshape(z_ref.shape[:3] + z.shape[1:])
            add_sums(st, z, cols)

        dot_tiles(h_ref, w_ref, emit)

    around(n, st, own, slots, ss_sem, sr_sem, tot_ref, work)


def sums_kernel(n, count, x_ref, tot_in, bn_ref, w_ref, u_ref, tot_ref, st, own, slots, ss_sem, sr_sem):
    def work():
        c = coefficients(tot_in, bn_ref, count)
        for k in range(x_ref.shape[0]):
            for r in range(x_ref.shape[1]):
                u_ref[k, r] = normed(x_ref[k, r], c).astype(BF)
        dot_tiles(u_ref, w_ref, lambda cols, z: add_sums(st, z, cols))

    around(n, st, own, slots, ss_sem, sr_sem, tot_ref, work)


def leave(u_ref, h_ref, tot_in, bn_ref, w_ref, o_ref, count):
    mean, scale, shift = coefficients(tot_in, bn_ref, count)

    def emit(cols, z):
        y = (z - mean[:, cols]) * scale[:, cols] + shift[:, cols]
        y = y + h_ref[:, :, :, cols].astype(F32).reshape(y.shape)
        o_ref[:, :, :, cols] = jnp.maximum(y, 0.0).astype(BF).reshape(o_ref.shape[:3] + y.shape[1:])

    dot_tiles(u_ref, w_ref, emit)


def leave_enter_kernel(n, count, u_ref, h_ref, tot_in, bn_ref, w_ref, w_next, o_ref, z_ref, tot_ref, st, own, slots, ss_sem, sr_sem):
    def work():
        leave(u_ref, h_ref, tot_in, bn_ref, w_ref, o_ref, count)

        def emit(cols, z):
            z_ref[:, :, :, cols] = z.reshape(z_ref.shape[:3] + z.shape[1:])
            add_sums(st, z, cols)

        dot_tiles(o_ref, w_next, emit)

    around(n, st, own, slots, ss_sem, sr_sem, tot_ref, work)


def leave_kernel(count, u_ref, h_ref, tot_in, bn_ref, w_ref, o_ref):
    leave(u_ref, h_ref, tot_in, bn_ref, w_ref, o_ref, count)


def point_call(n, kernel, collective_id, name, per_step, blocked, fixed, outs, sums, flops):
    images, rows, width = blocked[0].shape[:3]
    count = float(images * rows * width * n)
    block = lambda c: pl.BlockSpec((per_step, rows, width, c), lambda s: (s, 0, 0, 0))
    whole = lambda a: pl.BlockSpec(a.shape, lambda s: (0,) * a.ndim, pipeline_mode=pl.Buffered(1))
    out_specs = [block(c) for c, _ in outs]
    out_shape = [jax.ShapeDtypeStruct((images, rows, width, c), d) for c, d in outs]
    scratch = []
    if sums:
        out_specs.append(pl.BlockSpec((2, sums), lambda s: (0, 0)))
        out_shape.append(jax.ShapeDtypeStruct((2, sums), F32))
        scratch = [*sum_scratch(n, sums), pltpu.SemaphoreType.DMA((n - 1,)), pltpu.SemaphoreType.DMA((n - 1,))]
        kernel = functools.partial(kernel, n, count)
        params = pltpu.CompilerParams(collective_id=collective_id, has_side_effects=True, vmem_limit_bytes=VMEM)
    else:
        kernel = functools.partial(kernel, count)
        params = pltpu.CompilerParams(vmem_limit_bytes=VMEM)
    return pl.pallas_call(
        kernel,
        grid=(images // per_step,),
        in_specs=[block(a.shape[3]) for a in blocked] + [layer_spec(a) if isinstance(a, tuple) else whole(a) for a in fixed],
        out_specs=out_specs,
        out_shape=out_shape,
        scratch_shapes=scratch,
        compiler_params=params,
        cost_estimate=pl.CostEstimate(flops=flops, bytes_accessed=sum(a.nbytes for a in blocked), transcendentals=0),
        name=name,
    )(*blocked, *[a[0] if isinstance(a, tuple) else a for a in fixed])


def solution(mesh):
    n = mesh.shape["sp"]

    def forward(images, w_a, bn_a, w_down, bn_down, w_in, bn_in, w_mid, bn_mid, w_out, bn_out):
        layers, blocks = w_a.shape[0], w_in.shape[0]
        ids = itertools.count()
        bn_down = bn_down[None]
        z, tot = conv_layer(n, "a", 0, next(ids), images, None, w_a)
        for layer in range(1, layers):
            z, tot = conv_layer(n, "a", layer, next(ids), z, (tot, (bn_a, layer - 1)), w_a)
        z, tot = conv_layer(n, "down", 0, next(ids), z, (tot, (bn_a, layers - 1)), w_down)
        wide, slim = w_down.shape[-1], w_in.shape[-1]
        pixels = z.shape[0] * z.shape[1] * z.shape[2]
        flops = 2 * pixels * wide * slim
        hidden, z, tot = point_call(n, enter_kernel, next(ids), "enter", PER_STEP["enter"], [z], [tot, (bn_down, 0), (w_in, 0)], [(wide, BF), (slim, F32)], slim, flops)
        for block in range(blocks):
            z, tot = conv_layer(n, "mid", block, next(ids), z, (tot, (bn_in, block)), w_mid)
            branch, tot = point_call(n, sums_kernel, next(ids), "sums", PER_STEP["sums"], [z], [tot, (bn_mid, block), (w_out, block)], [(slim, BF)], wide, flops)
            fixed = [tot, (bn_out, block), (w_out, block)]
            if block + 1 < blocks:
                hidden, z, tot = point_call(n, leave_enter_kernel, next(ids), "leave_enter", PER_STEP["leave_enter"], [branch, hidden], fixed + [(w_in, block + 1)], [(wide, BF), (slim, F32)], slim, 2 * flops)
            else:
                hidden = point_call(n, leave_kernel, None, "leave", PER_STEP["leave"], [branch, hidden], fixed, [(wide, BF)], 0, flops)[0]
        return hidden

    act_spec = P("dp", "sp", None, None)
    return jax.shard_map(forward, mesh=mesh, in_specs=(act_spec,) + (P(),) * 10, out_specs=act_spec, check_vma=False)
```

time: 748 us -> 667 us (0.89)
  Pallas kernels: 715 us -> 661 us
  local copies, waits for them, and re-layouts: 24.7 us -> 0 us
    pallas_call x12, Pallas kernels: 715 us -> 661 us  [the longest x7 482 us: conv_layer(): pl.pallas_call(functools.partial(conv_kernel, n, images, kind, layer, mom...]
    slice x2 -> x0, local copies, waits for them, and re-layouts: 12.9 us -> none  [the longest x1 8.28 us: forward(): z, tot = conv_layer(n, 'mid', 4, z, (tot, bn_in[block]), w_mid[block])]
    squeeze x6 -> x0, local copies, waits for them, and re-layouts: 11.8 us -> none  [the longest x1 4.91 us: forward(): w_out[block]]
where the time goes in v2:
time: 667 us; the launch traced here: 662 us
  Pallas kernels  661 us (99%)
    pallas_call x7, Pallas kernels, conv_layer(): pl.pallas_call(functools.partial(conv_kernel, n, images, kind, layer, mom...  482 us
    pallas_call x5, Pallas kernels, point_call(): pl.pallas_call(kernel, grid=(images // per_step,), in_specs=[block(a.shap...  179 us

profile of v2, /device:TPU:0, one launch (start us, length us, event | category | flops | bytes accessed | tf_op | source)
XLA Modules:
  0.0 661.7 jit_solution(8938565103173688707)
XLA Ops:
  0.0 62.4 %conv_a.4 = (f32[16,4,512,256]{3,2,1,0:T(8,128)}, f32[2,256]{1,0:T(2,128)}) custom-call(bf16[16,4,512,256]{3,2,1,0:T(8,128)(2,1)} %refs_3_.1, bf16[16,4,512,256]{3,2,1,0:T(8,128)(2,1)} %refs_3_.1, bf16[16,4,512,256]{3,2,1,0:T(8,128)(2,1)} %refs_3_.1, bf16[16,4,512,256]{3,2,1,0:T(8,128)(2,1)} %refs_3_.1, bf16[4,2304,256]{2,1,0:T(8,128)(2,1)} %bitcast.8), custom_call_target="tpu_custom_call" | custom-call | flops 38654705664 | bytes 50331648 | tf_op jit(solution)/shard_map/conv_a/pallas_call | solution.py:304
  62.4 64.0 %conv_a.5 = (f32[16,4,512,256]{3,2,1,0:T(8,128)}, f32[2,256]{1,0:T(2,128)}) custom-call(f32[16,4,512,256]{3,2,1,0:T(8,128)} %get-tuple-element.29.refs_0_.refs_1_.refs_2_.refs_3_, f32[16,4,512,256]{3,2,1,0:T(8,128)} %get-tuple-element.29.refs_0_.refs_1_.refs_2_.refs_3_, f32[16,4,512,256]{3,2,1,0:T(8,128)} %get-tuple-element.29.refs_0_.refs_1_.refs_2_.refs_3_, ...), custom_call_target="tpu_custom_call" | custom-call | flops 38654705664 | bytes 67108864 | tf_op jit(solution)/shard_map/conv_a/pallas_call | solution.py:304
  126.5 65.0 %conv_a.6 = (f32[16,4,512,256]{3,2,1,0:T(8,128)}, f32[2,256]{1,0:T(2,128)}) custom-call(f32[16,4,512,256]{3,2,1,0:T(8,128)} %get-tuple-element.31.refs_0_.refs_1_.refs_2_.refs_3_, f32[16,4,512,256]{3,2,1,0:T(8,128)} %get-tuple-element.31.refs_0_.refs_1_.refs_2_.refs_3_, f32[16,4,512,256]{3,2,1,0:T(8,128)} %get-tuple-element.31.refs_0_.refs_1_.refs_2_.refs_3_, ...), custom_call_target="tpu_custom_call" | custom-call | flops 38654705664 | bytes 67108864 | tf_op jit(solution)/shard_map/conv_a/pallas_call | solution.py:304
  191.5 64.3 %conv_a.7 = (f32[16,4,512,256]{3,2,1,0:T(8,128)}, f32[2,256]{1,0:T(2,128)}) custom-call(f32[16,4,512,256]{3,2,1,0:T(8,128)} %get-tuple-element.33.refs_0_.refs_1_.refs_2_.refs_3_, f32[16,4,512,256]{3,2,1,0:T(8,128)} %get-tuple-element.33.refs_0_.refs_1_.refs_2_.refs_3_, f32[16,4,512,256]{3,2,1,0:T(8,128)} %get-tuple-element.33.refs_0_.refs_1_.refs_2_.refs_3_, ...), custom_call_target="tpu_custom_call" | custom-call | flops 38654705664 | bytes 67108864 | tf_op jit(solution)/shard_map/conv_a/pallas_call | solution.py:304
  255.8 103.1 %conv_down.1 = (f32[16,2,256,2048]{3,2,1,0:T(8,128)}, f32[2,2048]{1,0:T(2,128)}) custom-call(f32[16,4,512,256]{3,2,1,0:T(8,128)} %get-tuple-element.35.refs_0_.refs_1_.refs_2_, f32[16,4,512,256]{3,2,1,0:T(8,128)} %get-tuple-element.35.refs_0_.refs_1_.refs_2_, f32[16,4,512,256]{3,2,1,0:T(8,128)} %get-tuple-element.35.refs_0_.refs_1_.refs_2_, ...), custom_call_target="tpu_custom_call" | custom-call | flops 77309411328 | bytes 100663296 | tf_op jit(solution)/shard_map/conv_down/pallas_call | solution.py:304
  359.0 45.9 %enter.1 = (bf16[16,2,256,2048]{3,2,1,0:T(8,128)(2,1)}, f32[16,2,256,512]{3,2,1,0:T(8,128)}, f32[2,512]{1,0:T(2,128)}) custom-call(f32[16,2,256,2048]{3,2,1,0:T(8,128)} %get-tuple-element.37.x_ref, f32[2,2048]{1,0:T(2,128)} %get-tuple-element.38.tot_in, f32[1,2,2048]{2,1,0:T(2,128)} %bitcast.4, bf16[2,2048,512]{2,1,0:T(8,128)(2,1)} %w_next.1), custom_call_target="tpu_custom_call" | custom-call | flops 17179869184 | bytes 67108864 | tf_op jit(solution)/shard_map/enter/pallas_call | solution.py:432
  404.8 61.3 %conv_mid.2 = (f32[16,2,256,512]{3,2,1,0:T(8,128)}, f32[2,512]{1,0:T(2,128)}) custom-call(f32[16,2,256,512]{3,2,1,0:T(8,128)} %get-tuple-element.39.refs_0_.refs_1_.refs_2_.refs_3_, f32[16,2,256,512]{3,2,1,0:T(8,128)} %get-tuple-element.39.refs_0_.refs_1_.refs_2_.refs_3_, f32[16,2,256,512]{3,2,1,0:T(8,128)} %get-tuple-element.39.refs_0_.refs_1_.refs_2_.refs_3_, ...), custom_call_target="tpu_custom_call" | custom-call | flops 38654705664 | bytes 33554432 | tf_op jit(solution)/shard_map/conv_mid/pallas_call | solution.py:304
  466.1 25.9 %sums.2 = (bf16[16,2,256,512]{3,2,1,0:T(8,128)(2,1)}, f32[2,2048]{1,0:T(2,128)}) custom-call(f32[16,2,256,512]{3,2,1,0:T(8,128)} %get-tuple-element.41.x_ref, f32[2,512]{1,0:T(2,128)} %get-tuple-element.42.tot_in, f32[2,2,512]{2,1,0:T(2,128)} %bn_ref.6, bf16[2,512,2048]{2,1,0:T(8,128)(2,1)} %w_ref.9), custom_call_target="tpu_custom_call" | custom-call | flops 17179869184 | bytes 16777216 | tf_op jit(solution)/shard_map/sums/pallas_call | solution.py:432
  492.0 48.8 %leave_enter.1 = (bf16[16,2,256,2048]{3,2,1,0:T(8,128)(2,1)}, f32[16,2,256,512]{3,2,1,0:T(8,128)}, f32[2,512]{1,0:T(2,128)}) custom-call(bf16[16,2,256,512]{3,2,1,0:T(8,128)(2,1)} %get-tuple-element.43.u_ref, bf16[16,2,256,2048]{3,2,1,0:T(8,128)(2,1)} %get-tuple-element.44.h_ref, f32[2,2048]{1,0:T(2,128)} %get-tuple-element.45.tot_in, f32[2,2,2048]{2,1,0:T(2,128)} %bn_ref.7, ...), custom_call_target="tpu_custom_call" | custom-call | flops 34359738368 | bytes 41943040 | tf_op jit(solution)/shard_map/leave_enter/pallas_call | solution.py:432
  540.8 62.0 %conv_mid.3 = (f32[16,2,256,512]{3,2,1,0:T(8,128)}, f32[2,512]{1,0:T(2,128)}) custom-call(f32[16,2,256,512]{3,2,1,0:T(8,128)} %get-tuple-element.46.refs_0_.refs_1_.refs_2_.refs_3_, f32[16,2,256,512]{3,2,1,0:T(8,128)} %get-tuple-element.46.refs_0_.refs_1_.refs_2_.refs_3_, f32[16,2,256,512]{3,2,1,0:T(8,128)} %get-tuple-element.46.refs_0_.refs_1_.refs_2_.refs_3_, ...), custom_call_target="tpu_custom_call" | custom-call | flops 38654705664 | bytes 33554432 | tf_op jit(solution)/shard_map/conv_mid/pallas_call | solution.py:304
  602.8 25.3 %sums.3 = (bf16[16,2,256,512]{3,2,1,0:T(8,128)(2,1)}, f32[2,2048]{1,0:T(2,128)}) custom-call(f32[16,2,256,512]{3,2,1,0:T(8,128)} %get-tuple-element.48.x_ref, f32[2,512]{1,0:T(2,128)} %get-tuple-element.49.tot_in, f32[2,2,512]{2,1,0:T(2,128)} %bn_ref.6, bf16[2,512,2048]{2,1,0:T(8,128)(2,1)} %w_ref.9), custom_call_target="tpu_custom_call" | custom-call | flops 17179869184 | bytes 16777216 | tf_op jit(solution)/shard_map/sums/pallas_call | solution.py:432
  628.1 33.1 %leave.1 = bf16[16,2,256,2048]{3,2,1,0:T(8,128)(2,1)} custom-call(bf16[16,2,256,512]{3,2,1,0:T(8,128)(2,1)} %get-tuple-element.50.u_ref, bf16[16,2,256,2048]{3,2,1,0:T(8,128)(2,1)} %get-tuple-element.51.h_ref, f32[2,2048]{1,0:T(2,128)} %get-tuple-element.52.tot_in, f32[2,2,2048]{2,1,0:T(2,128)} %bn_ref.7, bf16[2,512,2048]{2,1,0:T(8,128)(2,1)} %w_ref.9), custom_call_target="tpu_custom_call" | custom-call | flops 17179869184 | bytes 41943040 | tf_op jit(solution)/shard_map/leave/pallas_call | solution.py:432
